TPU v7x, 16 devices: a whole 2x2x2 slice. The times are simulated.
16 devices in a mesh: rep: 1, dp: 16 (over x, y, z, core).
Axes of the slice: x: 2, y: 2, z: 2, core: 2. Of those that a mesh axis runs over, the one named last changes fastest.
Arguments:
- x: bfloat16 [16, 2048, 1280], P(('rep', 'dp'))
- dy: bfloat16 [16, 2048, 1280], P(('rep', 'dp'))
- w_gate: bfloat16 [2, 1280, 4480], P(None, 'dp')
- w_up: bfloat16 [2, 1280, 4480], P(None, 'dp')
- w_down: bfloat16 [2, 4480, 1280], P(None, 'dp')
Outputs:
- output 1: bfloat16 [16, 2048, 1280], P(('rep', 'dp'))
- output 2: bfloat16 [2, 1280, 4480], P('rep', 'dp')
- output 3: bfloat16 [2, 1280, 4480], P('rep', 'dp')
- output 4: bfloat16 [2, 4480, 1280], P('rep', 'dp')
All inputs are finite; a program needn't handle non-finite values.
Results may differ from a plain program's by a relative error of at most 0.018.
Values are sent between devices in bfloat16 or wider.
A program may use at most 2 GiB of HBM per device.

v0:
```python
import jax
import jax.numpy as jnp
from jax import lax

NAMES = ("w_gate", "w_up", "w_down")


def matmul(a, w):
    return jnp.dot(a, w, preferred_element_type=jnp.float32).astype(jnp.bfloat16)


def normed(h):
    wide = h.astype(jnp.float32)
    scale = lax.rsqrt(jnp.mean(wide**2, -1, keepdims=True) + 1e-6)
    return (wide * scale).astype(jnp.bfloat16)


def layer(h, w):
    a = normed(h)
    gate = jnp.dot(a, w["w_gate"], preferred_element_type=jnp.float32)
    up = jnp.dot(a, w["w_up"], preferred_element_type=jnp.float32)
    return h + matmul((jax.nn.silu(gate) * up).astype(jnp.bfloat16), w["w_down"])


def stack(weights, h):
    for number in range(weights["w_gate"].shape[0]):
        h = layer(h, {name: w[number] for name, w in weights.items()})
    return h


def solution(mesh):
    groups = mesh.shape["rep"]

    def step(x, dy, *weights):
        shape = x.shape
        x, dy = (t.reshape(groups, -1, *t.shape[1:]) for t in (x, dy))

        def of_a_group(x, dy):
            _, back = jax.vjp(stack, dict(zip(NAMES, weights, strict=True)), x)
            by_weights, by_x = back(dy)
            return (by_x, *(by_weights[name] for name in NAMES))

        by_x, *by_weights = jax.vmap(of_a_group)(x, dy)
        return (by_x.reshape(shape), *(t.reshape(-1, *t.shape[2:]) for t in by_weights))

    return step
```

profile of v0, /device:TPU:0, one launch (start us, length us, event | category | flops | bytes accessed | tf_op | source)
XLA Modules:
  0.0 2694.7 jit_solution(12129968489676305421)
XLA Ops:
  47.7 228.7 %while.13 = (bf16[1,2048,1280]{2,1,0:T(8,128)(2,1)}, bf16[1,280,1280]{2,1,0:T(8,128)(2,1)}, bf16[1,2048,4480]{1,2,0:T(8,128)(2,1)}, bf16[1,280,1280]{2,1,0:T(8,1...) while((bf16[1,2048,1280]{2,1,0:T(8,128)(2,1)}, ...), condition=%wide.windowed_dot_general_cond_ag, body=%wide.windowed_dot_general_body_ag.sunk | while | flops 5873459200 | bytes 38584860 | solution.py:9
  103.0 17.7 collective-permute-start.2
  157.8 22.0 collective-permute-done.3
  276.4 22.4 copy.2
  298.8 32.4 %fusion.194 = f32[2048,4480]{1,0:T(8,128)} fusion(bf16[1,1280,4480]{2,1,0:T(8,128)(2,1)} %all-gather.27.cloned.1.call-done, bf16[1,2048,1280]{1,2,0:T(8,128)(2,1)} %fusion.201), kind=kOutput, calls=%fused_computation.247 | convolution fusion | flops 23488102400 | bytes 53411840 | tf_op jit(solution)/vmap(jvp())/dot_general | solution.py:20
  331.2 45.8 %fusion.176 = (bf16[1,2048,4480]{2,1,0:T(8,128)(2,1)}, f32[2048,4480]{1,0:T(8,128)}) fusion(f32[2048,4480]{1,0:T(8,128)} %fusion.194, bf16[1,1280,4480]{2,1,0:T(8,128)(2,1)} %all-gather.29.cloned.1.call-done, bf16[1,2048,1280]{1,2,0:T(8,128)(2,1)} %fusion.201), kind=kOutput, calls=%fused_computation.215 | convolution fusion | flops 23543152640 | bytes 108462080 | tf_op jit(solution)/vmap(jvp())/dot_general | solution.py:21
  377.1 24.6 copy.6
  401.7 33.2 %fusion.203 = (f32[2048]{0:T(1024)S(1)}, bf16[1,2048,1280]{1,2,0:T(8,128)(2,1)}) fusion(bf16[1,2048,1280]{1,2,0:T(8,128)(2,1)} %copy.1, bf16[1,4480,1280]{2,1,0:T(8,128)(2,1)} %all-gather.31.cloned.1.call-done, bf16[1,2048,4480]{2,1,0:T(8,128)(2,1)} %get-tuple-element.281), kind=kOutput, calls=%fused_computation.256 | convolution fusion | flops 23501207552 | bytes 40312832 | tf_op jit(solution)/vmap(jvp())/dot_general | solution.py:9
  442.7 31.8 %fusion.186 = f32[2048,4480]{1,0:T(8,128)} fusion(bf16[1,1280,4480]{2,1,0:T(8,128)(2,1)} %all-gather.33.cloned.1.call-done, bf16[1,2048,1280]{1,2,0:T(8,128)(2,1)} %fusion.204), kind=kOutput, calls=%fused_computation.239 | convolution fusion | flops 23488102400 | bytes 53411840 | tf_op jit(solution)/vmap(jvp())/dot_general | solution.py:20
  474.6 45.9 %fusion.170 = (bf16[1,2048,4480]{2,1,0:T(8,128)(2,1)}, f32[2048,4480]{1,0:T(8,128)}) fusion(f32[2048,4480]{1,0:T(8,128)} %fusion.186, bf16[1,1280,4480]{2,1,0:T(8,128)(2,1)} %all-gather.35.cloned.1.call-done, bf16[1,2048,1280]{1,2,0:T(8,128)(2,1)} %fusion.204), kind=kOutput, calls=%fused_computation.205 | convolution fusion | flops 23543152640 | bytes 108462080 | tf_op jit(solution)/vmap(jvp())/dot_general | solution.py:21
  520.4 24.7 copy.4
  545.2 293.0 %while.18 = (bf16[1,2048,4480]{1,2,0:T(8,128)(2,1)}, bf16[1,2048,1280]{2,1,0:T(8,128)(2,1)}, f32[280,1280]{1,0:T(8,128)S(1)}, f32[280,1280]{1,0:T(8,128)}, u32[]...) while((bf16[1,2048,4480]{1,2,0:T(8,128)(2,1)}, ...), condition=%wide.windowed_dot_general_cond_rs.4.clone, body=%wide.windowed_dot_general_body_rs.4.clone.sunk | while | flops 5883351040 | bytes 98796104 | solution.py:9
  617.8 16.6 collective-permute-start.20
  854.3 38.0 %fusion.161 = (bf16[1,2048,4480]{2,1,0:T(8,128)(2,1)S(1)}, bf16[1,2048,4480]{2,1,0:T(8,128)(2,1)}) fusion(f32[2048,4480]{1,0:T(8,128)} %fusion.186, f32[2048,4480]{1,0:T(8,128)} %get-tuple-element.290, bf16[1,2048,4480]{2,1,0:T(8,128)(2,1)} %copy.2), kind=kLoop, calls=%fused_computation.195 | loop fusion | flops 137625600 | bytes 128450560 | tf_op jit(solution)/vmap(transpose(jvp(jit(silu))))/add_any | solution.py:22
  892.3 38.6 %fusion.211 = bf16[2048,1280]{0,1:T(8,128)(2,1)} fusion(bf16[1,1280,4480]{2,1,0:T(8,128)(2,1)} %all-gather.35.cloned.1.call-done, bf16[1,2048,4480]{2,1,0:T(8,128)(2,1)} %get-tuple-element.694), kind=kOutput, calls=%fused_computation.260 | convolution fusion | flops 23488102400 | bytes 35061760 | tf_op jit(solution)/vmap(transpose(jvp()))/dot_general | solution.py:21
  930.9 29.8 %fusion.205 = (f32[2048]{0:T(1024)S(1)}, bf16[1,2048,1280]{1,2,0:T(8,128)(2,1)}) fusion(bf16[1,2048,1280]{1,2,0:T(8,128)(2,1)} %get-tuple-element.284, bf16[2048,1280]{0,1:T(8,128)(2,1)} %fusion.211, bf16[1,1280,4480]{2,1,0:T(8,128)(2,1)} %all-gather.33.cloned.1.call-done, bf16[1,2048,4480]{2,1,0:T(8,128)(2,1)S(1)} %get-tuple-element.622), kind=kOutput, calls=%fused_computation.258 | convolution fusion | flops 23501207552 | bytes 45555712 | tf_op jit(solution)/vmap(transpose(jvp()))/dot_general | solution.py:20
  981.1 298.6 %while.19 = (bf16[1,2048,1280]{2,1,0:T(8,128)(2,1)}, bf16[1,2048,4480]{1,2,0:T(8,128)(2,1)}, f32[1280,280]{0,1:T(8,128)S(1)}, f32[1280,280]{0,1:T(8,128)}, u32[]...) while((bf16[1,2048,1280]{2,1,0:T(8,128)(2,1)}, ...), condition=%wide.windowed_dot_general_cond_rs.5.clone, body=%wide.windowed_dot_general_body_rs.5.clone.sunk | while | flops 5883351040 | bytes 98796104 | solution.py:9
  1006.8 29.5 %collective-permute-start.26 = (f32[1280,280]{0,1:T(8,128)}, f32[1280,280]{0,1:T(8,128)}, u32[]{:S(2)}, u32[]{:S(2)}) collective-permute-start(f32[1280,280]{0,1:T(8,128)} %get-tuple-element.552), channel_id=51, source_target_pairs={{0,1},{1,2},{2,3},{3,4},{4,5},{5,6},{6,7},{7,8},{8,9},{9,10},{10,1... | collective-permute-start | bytes 4300808 | tf_op jit(solution)/vmap(transpose(jvp()))/dot_general | solution.py:9
  1295.8 295.3 %while.16 = (bf16[1,2048,4480]{2,1,0:T(8,128)(2,1)}, bf16[1,2048,1280]{1,2,0:T(8,128)(2,1)}, f32[4480,80]{0,1:T(8,128)S(1)}, f32[4480,80]{0,1:T(8,128)}, u32[]{:...) while((bf16[1,2048,4480]{2,1,0:T(8,128)(2,1)}, ...), condition=%wide.windowed_dot_general_cond_rs.2.clone, body=%wide.windowed_dot_general_body_rs.2.clone.sunk | while | flops 5876797440 | bytes 98796104 | solution.py:21
  1320.9 30.5 %collective-permute-start.14 = (f32[4480,80]{0,1:T(8,128)}, f32[4480,80]{0,1:T(8,128)S(1)}, u32[]{:S(2)}, u32[]{:S(2)}) collective-permute-start(f32[4480,80]{0,1:T(8,128)} %get-tuple-element.525), channel_id=33, source_target_pairs={{0,1},{1,2},{2,3},{3,4},{4,5},{5,6},{6,7},{7,8},{8,9},{9,10},{10,1... | collective-permute-start | bytes 4300808 | tf_op jit(solution)/vmap(transpose(jvp()))/dot_general | solution.py:21
  1445.5 16.8 collective-permute-start.12
  1519.5 16.8 collective-permute-start.12
  1591.2 16.8 collective-permute-start.31
  1607.9 52.1 %fusion.163 = (bf16[1,2048,4480]{2,1,0:T(8,128)(2,1)}, bf16[1,2048,4480]{2,1,0:T(8,128)(2,1)}) fusion(f32[2048,4480]{1,0:T(8,128)} %fusion.194, f32[2048,4480]{1,0:T(8,128)} %get-tuple-element.282, bf16[1,4480,1280]{2,1,0:T(8,128)(2,1)} %all-gather.31.cloned.1.call-done, bf16[1,2048,1280]{1,2,0:T(8,128)(2,1)} %fusion.262), kind=kOutput, calls=%fused_computation.197 | convolution fusion | flops 23634903040 | bytes 126812160 | tf_op jit(solution)/vmap(transpose(jvp()))/dot_general | solution.py:9
  1660.1 298.3 %while.17 = (bf16[1,2048,4480]{2,1,0:T(8,128)(2,1)}, bf16[1,2048,1280]{1,2,0:T(8,128)(2,1)}, f32[4480,80]{0,1:T(8,128)S(1)}, f32[4480,80]{0,1:T(8,128)}, u32[]{:...) while((bf16[1,2048,4480]{2,1,0:T(8,128)(2,1)}, ...), condition=%wide.windowed_dot_general_cond_rs.3.clone, body=%wide.windowed_dot_general_body_rs.3.clone.sunk | while | flops 5876797440 | bytes 98796104 | solution.py:21
  1685.9 29.5 %collective-permute-start.18 = (f32[4480,80]{0,1:T(8,128)}, f32[4480,80]{0,1:T(8,128)}, u32[]{:S(2)}, u32[]{:S(2)}) collective-permute-start(f32[4480,80]{0,1:T(8,128)} %get-tuple-element.534), channel_id=39, source_target_pairs={{0,1},{1,2},{2,3},{3,4},{4,5},{5,6},{6,7},{7,8},{8,9},{9,10},{10,1... | collective-permute-start | bytes 4300808 | tf_op jit(solution)/vmap(transpose(jvp()))/dot_general | solution.py:21
  1885.4 16.3 collective-permute-start.16
  1959.4 294.8 %while.14 = (bf16[1,2048,4480]{2,1,0:T(8,128)(2,1)}, bf16[1,2048,1280]{1,2,0:T(8,128)(2,1)}, f32[4480,80]{0,1:T(8,128)S(1)}, f32[4480,80]{0,1:T(8,128)}, u32[]{:...) while((bf16[1,2048,4480]{2,1,0:T(8,128)(2,1)}, ...), condition=%wide.windowed_dot_general_cond_rs.clone, body=%wide.windowed_dot_general_body_rs.clone.sunk | while | flops 5876797440 | bytes 98796104 | solution.py:20
  2255.4 295.6 %while.15 = (bf16[1,2048,4480]{2,1,0:T(8,128)(2,1)}, bf16[1,2048,1280]{1,2,0:T(8,128)(2,1)}, f32[4480,80]{0,1:T(8,128)}, f32[4480,80]{0,1:T(8,128)}, u32[]{:T(12...) while((bf16[1,2048,4480]{2,1,0:T(8,128)(2,1)}, ...), condition=%wide.windowed_dot_general_cond_rs.1.clone, body=%wide.windowed_dot_general_body_rs.1.clone.sunk | while | flops 5876797440 | bytes 98796104 | solution.py:20
  2403.4 16.3 collective-permute-start.8
  2567.1 32.0 %fusion.221 = bf16[2048,1280]{0,1:T(8,128)(2,1)} fusion(bf16[1,1280,4480]{2,1,0:T(8,128)(2,1)} %all-gather.29.cloned.1.call-done, bf16[1,2048,4480]{2,1,0:T(8,128)(2,1)} %get-tuple-element.808), kind=kOutput, calls=%fused_computation.262 | convolution fusion | flops 23488102400 | bytes 35061760 | tf_op jit(solution)/vmap(transpose(jvp()))/dot_general | solution.py:21
  2599.2 29.9 %fusion.202 = (f32[2048]{0:T(1024)S(1)}, bf16[1,2048,1280]{1,2,0:T(8,128)(2,1)}) fusion(bf16[1,2048,1280]{1,2,0:T(8,128)(2,1)} %copy.1, bf16[2048,1280]{0,1:T(8,128)(2,1)} %fusion.221, bf16[1,1280,4480]{2,1,0:T(8,128)(2,1)} %all-gather.27.cloned.1.call-done, bf16[1,2048,4480]{2,1,0:T(8,128)(2,1)S(1)} %bitcast.610), kind=kOutput, calls=%fused_computation.255 | convolution fusion | flops 23501207552 | bytes 45555712 | tf_op jit(solution)/vmap(transpose(jvp()))/dot_general | solution.py:20
  (515 shorter events, 1967.7 us)
Async XLA Ops:
  7.2 291.7 %all-gather.27.cloned.1.call-start = ((), (), s32[]{:S(2)}) async-start(), calls=%async_computation | async-start | bytes 12185600 | tf_op jit(solution)/vmap(jvp())/squeeze | solution.py:27
  10.0 321.3 %all-gather.29.cloned.1.call-start = ((), (), s32[]{:S(2)}) async-start(), calls=%async_computation.1 | async-start | bytes 12185600 | tf_op jit(solution)/vmap(jvp())/squeeze | solution.py:27
  11.2 390.4 %all-gather.31.cloned.1.call-start = ((), (), s32[]{:S(2)}) async-start(), calls=%async_computation.2 | async-start | bytes 12185600 | tf_op jit(solution)/vmap(jvp())/squeeze | solution.py:27
  13.0 429.7 %all-gather.33.cloned.1.call-start = ((), (), s32[]{:S(2)}) async-start(), calls=%async_computation.3 | async-start | bytes 12185600 | tf_op jit(solution)/vmap(jvp())/squeeze | solution.py:27
  13.6 460.9 %all-gather.35.cloned.1.call-start = ((), (), s32[]{:S(2)}) async-start(), calls=%async_computation.4 | async-start | bytes 12185600 | tf_op jit(solution)/vmap(jvp())/squeeze | solution.py:27
  13.7 27.5 %collective-permute-start.28 = (bf16[1,280,1280]{2,1,0:T(8,128)(2,1)}, bf16[1,280,1280]{2,1,0:T(8,128)(2,1)}, u32[]{:S(2)}, u32[]{:S(2)}) collective-permute-start(bf16[1,280,1280]{2,1,0:T(8,128)(2,1)} %get-tuple-element.557), channel_id=6, source_target_pairs={{0,1},{1,2},{2,3},{3,4},{4,5},{5,6},{6,7},{7,8},{8,9},{9,10},{10,1... | collective-permute-start | bytes 2150408 | tf_op jit(solution)/vmap(transpose(jvp()))/dot_general | solution.py:9
  47.7 28.5 %collective-permute-start = (bf16[1,280,1280]{2,1,0:T(8,128)(2,1)}, bf16[1,280,1280]{2,1,0:T(8,128)(2,1)S(1)}, u32[]{:S(2)}, u32[]{:S(2)}) collective-permute-start(bf16[1,280,1280]{2,1,0:T(8,128)(2,1)} %get-tuple-element.567), channel_id=7, source_target_pairs={{0,15},{1,0},{2,1},{3,2},{4,3},{5,4},{6,5},{7,6},{8,7},{9,8},{10,9... | collective-permute-start | bytes 2150408 | tf_op jit(solution)/vmap(transpose(jvp()))/dot_general | solution.py:9
  52.1 27.8 %collective-permute-start.2 = (bf16[1,280,1280]{2,1,0:T(8,128)(2,1)}, bf16[1,280,1280]{2,1,0:T(8,128)(2,1)}, u32[]{:S(2)}, u32[]{:S(2)}) collective-permute-start(bf16[1,280,1280]{2,1,0:T(8,128)(2,1)} %get-tuple-element.569), channel_id=8, source_target_pairs={{0,1},{1,2},{2,3},{3,4},{4,5},{5,6},{6,7},{7,8},{8,9},{9,10},{10,1... | collective-permute-start | bytes 2150408 | tf_op jit(solution)/vmap(transpose(jvp()))/dot_general | solution.py:9
  99.7 29.2 %collective-permute-start = (bf16[1,280,1280]{2,1,0:T(8,128)(2,1)}, bf16[1,280,1280]{2,1,0:T(8,128)(2,1)S(1)}, u32[]{:S(2)}, u32[]{:S(2)}) collective-permute-start(bf16[1,280,1280]{2,1,0:T(8,128)(2,1)} %get-tuple-element.567), channel_id=7, source_target_pairs={{0,15},{1,0},{2,1},{3,2},{4,3},{5,4},{6,5},{7,6},{8,7},{9,8},{10,9... | collective-permute-start | bytes 2150408 | tf_op jit(solution)/vmap(transpose(jvp()))/dot_general | solution.py:9
  103.0 37.2 %collective-permute-start.2 = (bf16[1,280,1280]{2,1,0:T(8,128)(2,1)}, bf16[1,280,1280]{2,1,0:T(8,128)(2,1)}, u32[]{:S(2)}, u32[]{:S(2)}) collective-permute-start(bf16[1,280,1280]{2,1,0:T(8,128)(2,1)} %get-tuple-element.569), channel_id=8, source_target_pairs={{0,1},{1,2},{2,3},{3,4},{4,5},{5,6},{6,7},{7,8},{8,9},{9,10},{10,1... | collective-permute-start | bytes 2150408 | tf_op jit(solution)/vmap(transpose(jvp()))/dot_general | solution.py:9
  128.9 28.9 %collective-permute-start.1 = (bf16[1,280,1280]{2,1,0:T(8,128)(2,1)S(1)}, bf16[1,280,1280]{2,1,0:T(8,128)(2,1)}, u32[]{:S(2)}, u32[]{:S(2)}) collective-permute-start(bf16[1,280,1280]{2,1,0:T(8,128)(2,1)S(1)} %collective-permute-done), channel_id=9, source_target_pairs={{0,15},{1,0},{2,1},{3,2},{4,3},{5,4},{6,5},{7,6},{8,7},{9,8},{10,9... | collective-permute-start | bytes 2150408 | tf_op jit(solution)/vmap(transpose(jvp()))/dot_general | solution.py:9
  146.0 33.8 %collective-permute-start.3 = (bf16[1,280,1280]{2,1,0:T(8,128)(2,1)}, bf16[1,280,1280]{2,1,0:T(8,128)(2,1)}, u32[]{:S(2)}, u32[]{:S(2)}) collective-permute-start(bf16[1,280,1280]{2,1,0:T(8,128)(2,1)} %collective-permute-done.2), channel_id=10, source_target_pairs={{0,1},{1,2},{2,3},{3,4},{4,5},{5,6},{6,7},{7,8},{8,9},{9,10},{10,1... | collective-permute-start | bytes 2150408 | tf_op jit(solution)/vmap(transpose(jvp()))/dot_general | solution.py:9
  199.6 25.3 collective-permute-start.3
  240.7 26.4 collective-permute-start.1
  250.3 26.1 collective-permute-start.3
  838.2 1816.2 %collective-permute-start.33 = (f32[280,1280]{1,0:T(8,128)}, f32[280,1280]{1,0:T(8,128)}, u32[]{:S(2)}, u32[]{:S(2)}) collective-permute-start(f32[280,1280]{1,0:T(8,128)} %get-tuple-element.52), channel_id=46, source_target_pairs={{0,1},{1,2},{2,3},{3,4},{4,5},{5,6},{6,7},{7,8},{8,9},{9,10},{10,1... | collective-permute-start | bytes 4300808 | tf_op jit(solution)/vmap(transpose(jvp()))/dot_general | solution.py:9
  1006.8 35.8 %collective-permute-start.26 = (f32[1280,280]{0,1:T(8,128)}, f32[1280,280]{0,1:T(8,128)}, u32[]{:S(2)}, u32[]{:S(2)}) collective-permute-start(f32[1280,280]{0,1:T(8,128)} %get-tuple-element.552), channel_id=51, source_target_pairs={{0,1},{1,2},{2,3},{3,4},{4,5},{5,6},{6,7},{7,8},{8,9},{9,10},{10,1... | collective-permute-start | bytes 4300808 | tf_op jit(solution)/vmap(transpose(jvp()))/dot_general | solution.py:9
  1279.8 1377.9 %collective-permute-start.34 = (f32[1280,280]{0,1:T(8,128)}, f32[1280,280]{0,1:T(8,128)}, u32[]{:S(2)}, u32[]{:S(2)}) collective-permute-start(f32[1280,280]{0,1:T(8,128)} %get-tuple-element.54), channel_id=52, source_target_pairs={{0,1},{1,2},{2,3},{3,4},{4,5},{5,6},{6,7},{7,8},{8,9},{9,10},{10,1... | collective-permute-start | bytes 4300808 | tf_op jit(solution)/vmap(transpose(jvp()))/dot_general | solution.py:9
  1320.9 38.6 %collective-permute-start.14 = (f32[4480,80]{0,1:T(8,128)}, f32[4480,80]{0,1:T(8,128)S(1)}, u32[]{:S(2)}, u32[]{:S(2)}) collective-permute-start(f32[4480,80]{0,1:T(8,128)} %get-tuple-element.525), channel_id=33, source_target_pairs={{0,1},{1,2},{2,3},{3,4},{4,5},{5,6},{6,7},{7,8},{8,9},{9,10},{10,1... | collective-permute-start | bytes 4300808 | tf_op jit(solution)/vmap(transpose(jvp()))/dot_general | solution.py:21
  1445.5 25.1 collective-permute-start.12
  1519.5 25.1 collective-permute-start.12
  1591.2 1061.6 %collective-permute-start.31 = (f32[4480,80]{0,1:T(8,128)}, f32[4480,80]{0,1:T(8,128)}, u32[]{:S(2)}, u32[]{:S(2)}) collective-permute-start(f32[4480,80]{0,1:T(8,128)} %get-tuple-element.48), channel_id=34, source_target_pairs={{0,1},{1,2},{2,3},{3,4},{4,5},{5,6},{6,7},{7,8},{8,9},{9,10},{10,1... | collective-permute-start | bytes 4300808 | tf_op jit(solution)/vmap(transpose(jvp()))/dot_general | solution.py:21
  1685.9 37.6 %collective-permute-start.18 = (f32[4480,80]{0,1:T(8,128)}, f32[4480,80]{0,1:T(8,128)}, u32[]{:S(2)}, u32[]{:S(2)}) collective-permute-start(f32[4480,80]{0,1:T(8,128)} %get-tuple-element.534), channel_id=39, source_target_pairs={{0,1},{1,2},{2,3},{3,4},{4,5},{5,6},{6,7},{7,8},{8,9},{9,10},{10,1... | collective-permute-start | bytes 4300808 | tf_op jit(solution)/vmap(transpose(jvp()))/dot_general | solution.py:21
  1810.1 25.4 collective-permute-start.16
  1885.4 25.6 collective-permute-start.16
  2070.5 24.4 collective-permute-start.6
  2255.7 24.4 collective-permute-start.8
  2329.0 25.8 collective-permute-start.8
  2403.4 26.0 collective-permute-start.8
  2478.0 25.8 collective-permute-start.8
  2551.0 105.1 %collective-permute-start.32 = (f32[4480,80]{0,1:T(8,128)}, f32[4480,80]{0,1:T(8,128)}, u32[]{:S(2)}, u32[]{:S(2)}) collective-permute-start(f32[4480,80]{0,1:T(8,128)} %get-tuple-element.50), channel_id=40, source_target_pairs={{0,1},{1,2},{2,3},{3,4},{4,5},{5,6},{6,7},{7,8},{8,9},{9,10},{10,1... | collective-permute-start | bytes 4300808 | tf_op jit(solution)/vmap(transpose(jvp()))/dot_general | solution.py:21
  2652.8 32.2 %collective-permute-start.30 = (f32[4480,80]{0,1:T(8,128)S(1)}, f32[4480,80]{0,1:T(8,128)S(1)}, u32[]{:S(2)}, u32[]{:S(2)}) collective-permute-start(f32[4480,80]{0,1:T(8,128)S(1)} %copy-done.16), channel_id=28, source_target_pairs={{0,1},{1,2},{2,3},{3,4},{4,5},{5,6},{6,7},{7,8},{8,9},{9,10},{10,1... | collective-permute-start | bytes 4300808 | tf_op jit(solution)/vmap(transpose(jvp()))/dot_general | solution.py:20
  (124 other events, 3027.9 us)
Sparse Core Ops, SparseCore 0:
  10.2 85.4 all-gather.26
  97.9 101.9 all-gather.28
  202.2 93.2 all-gather.30
  297.5 58.2 all-gather.32
  357.9 58.7 all-gather.34
where the time goes:
time: 2710 us; the launch traced here: 2690 us
  starting transfers between devices  926 us (34%)
  matrix products  781 us (29%)
  waiting for transfers between devices  524 us (19%)
  other arithmetic  308 us (11%)
  local copies, waits for them, and re-layouts  138 us (5%)
    dot_general x51, starting transfers between devices, matmul(): jnp.dot(a, w, preferred_element_type=jnp.float32).astype(jnp.bfloat16)  377 us
    dot_general x20, matrix products, layer(): up = jnp.dot(a, w['w_up'], preferred_element_type=jnp.float32)  293 us
    dot_general x34, starting transfers between devices, layer(): up = jnp.dot(a, w['w_up'], preferred_element_type=jnp.float32)  288 us
    dot_general x34, starting transfers between devices, layer(): gate = jnp.dot(a, w['w_gate'], preferred_element_type=jnp.float32)  260 us
    dot_general x20, matrix products, layer(): gate = jnp.dot(a, w['w_gate'], preferred_element_type=jnp.float32)  254 us
    dot_general x51, waiting for transfers between devices, matmul(): jnp.dot(a, w, preferred_element_type=jnp.float32).astype(jnp.bfloat16)  235 us
    dot_general x26, matrix products, matmul(): jnp.dot(a, w, preferred_element_type=jnp.float32).astype(jnp.bfloat16)  234 us
    dot_general x34, waiting for transfers between devices, layer(): gate = jnp.dot(a, w['w_gate'], preferred_element_type=jnp.float32)  156 us
  transfers between devices with their start and end apart: 124, of which 60 were waited for; matrix products, arithmetic and copies ran while one was open for 41% of the time, Pallas kernels for 0%

commit v1 on v0

v1 whole, which is shorter than its diff:
```python
import jax
import jax.numpy as jnp
from jax import lax
from jax.experimental import pallas as pl
from jax.experimental.pallas import tpu as pltpu
from jax.sharding import PartitionSpec as P

EPS = 1e-6
BF = jnp.bfloat16
F32 = jnp.float32
MESH = pl.DeviceIdType.MESH
ORDERS = ((0, 1, 2), (1, 2, 0), (2, 0, 1))
LAGS = (1, 3, 5, 6)


def gather_all(shards):
    parts = []
    for i, s in enumerate(shards):
        step = 512 if s.shape[1] > s.shape[0] * 16 else 256
        parts += [(i, c0, min(step, s.shape[1] - c0)) for c0 in range(0, s.shape[1], step)]
    n, total = len(shards), len(parts)

    def kernel(*refs):
        srcs, dsts, stage = refs[:n], refs[n : 2 * n], refs[2 * n : 3 * n]
        local, sent, got = refs[3 * n :]
        me = lax.axis_index("dp")
        core, xyz = me % 2, (me // 8, (me // 4) % 2, (me // 2) % 2)
        near = [me + 8 * (1 - 2 * xyz[0]), me + 4 * (1 - 2 * xyz[1]), me + 2 * (1 - 2 * xyz[2]), me + (1 - 2 * core)]
        whole = dsts
        ins = [pltpu.make_async_copy(srcs[i], stage[i], local.at[i]) for i in range(n)]
        for c in ins:
            c.start()
        barrier = pltpu.get_barrier_semaphore()
        for d in near:
            pl.semaphore_signal(barrier, inc=1, device_id={"dp": d}, device_id_type=MESH)
        for c in ins:
            c.wait()
        own = [pltpu.make_async_copy(stage[i], whole[i].at[(*xyz, core)], local.at[i]) for i in range(n)]
        for c in own:
            c.start()
        pl.semaphore_wait(barrier, 4)

        def hop(p, r):
            i, c0, width = parts[p]
            order = ORDERS[p % 3]
            at = list(xyz)
            for k in range(min(r, 3)):
                at[order[k]] = slice(None)
            there = whole[i].at[at[0], at[1], at[2], core, :, pl.ds(c0, width)]
            here = stage[i].at[:, pl.ds(c0, width)] if r == 0 else there
            return pltpu.make_async_remote_copy(
                here, there, sent.at[p, r], got.at[p, r],
                device_id={"dp": near[3] if r == 3 else near[order[r]]}, device_id_type=MESH)

        for t in range(total + LAGS[3] + 1):
            if t == LAGS[0]:
                for c in own:
                    c.wait()
            if t < total:
                hop(t, 0).start()
            for r in range(4):
                p = t - LAGS[r]
                if 0 <= p < total:
                    hop(p, r).wait_recv()
                    if r < 3:
                        hop(p, r + 1).start()
        for p in range(total):
            for r in range(4):
                hop(p, r).wait_send()

    made = pl.pallas_call(
        kernel,
        out_shape=[jax.ShapeDtypeStruct((2, 2, 2, 2, *s.shape), s.dtype) for s in shards],
        in_specs=[pl.BlockSpec(memory_space=pl.ANY)] * n,
        out_specs=[pl.BlockSpec(memory_space=pl.ANY)] * n,
        scratch_shapes=[pltpu.VMEM(s.shape, s.dtype) for s in shards]
        + [pltpu.SemaphoreType.DMA((n,)), pltpu.SemaphoreType.DMA((total, 4)), pltpu.SemaphoreType.DMA((total, 4))],
        compiler_params=pltpu.CompilerParams(collective_id=0, has_side_effects=True, vmem_limit_bytes=40 * 2**20),
        name="gather_all",
    )(*shards)
    return [t.reshape(-1, t.shape[-1]) for t in made]


def norm_stats(h):
    wide = h.astype(F32)
    scale = lax.rsqrt(jnp.mean(wide**2, -1, keepdims=True) + EPS)
    return wide, scale


def dot(a, b, dims):
    return lax.dot_general(a, b, (dims, ((), ())), preferred_element_type=F32)


def solution(mesh):
    def body(x, dy, wg, wu, wd):
        x, dy = x[0], dy[0]
        layers = wg.shape[0]
        whole = gather_all([w[i] for i in range(layers) for w in (wg, wu, wd)])
        g_w, u_w, d_w = whole[0::3], whole[1::3], whole[2::3]
        saved = []
        h = x
        for i in range(layers):
            wide, scale = norm_stats(h)
            a = (wide * scale).astype(BF)
            gate = dot(a, g_w[i], ((1,), (0,)))
            up = dot(a, u_w[i], ((1,), (0,)))
            act = (jax.nn.silu(gate) * up).astype(BF)
            saved.append((h, a, gate, up, act))
            if i < layers - 1:
                h = h + dot(act, d_w[i], ((1,), (0,))).astype(BF)
        ct = dy
        out_g, out_u, out_d = [None] * layers, [None] * layers, [None] * layers
        scatter = lambda t: lax.psum_scatter(t.astype(BF), "dp", scatter_dimension=0, tiled=True)
        for i in reversed(range(layers)):
            h, a, gate, up, act = saved[i]
            dact = dot(ct, d_w[i], ((1,), (1,))).astype(BF)
            out_d[i] = scatter(dot(act, ct, ((0,), (0,))))
            da32 = dact.astype(F32)
            sig = jax.nn.sigmoid(gate)
            silu = gate * sig
            dup = (da32 * silu).astype(BF)
            dgate = (da32 * up * (sig * (1 + gate * (1 - sig)))).astype(BF)
            out_g[i] = scatter(dot(a, dgate, ((0,), (0,))))
            out_u[i] = scatter(dot(a, dup, ((0,), (0,))))
            da = dot(dgate, g_w[i], ((1,), (1,))).astype(BF) + dot(dup, u_w[i], ((1,), (1,))).astype(BF)
            wide, scale = norm_stats(h)
            daw = da.astype(F32)
            inner = jnp.mean(daw * wide, -1, keepdims=True)
            dh = daw * scale - wide * (scale**3 * inner)
            ct = ct + dh.astype(BF)
        return (ct[None], jnp.stack(out_g), jnp.stack(out_u), jnp.stack(out_d))

    return jax.shard_map(
        body, mesh=mesh,
        in_specs=(P(("rep", "dp")), P(("rep", "dp")), P(None, "dp"), P(None, "dp"), P(None, "dp")),
        out_specs=(P(("rep", "dp")), P("rep", "dp"), P("rep", "dp"), P("rep", "dp")),
        check_vma=False)
```

time: 2710 us -> 1380 us (0.51)
  starting transfers between devices: 926 us -> 0.25 us
  other arithmetic: 308 us -> 36.1 us
  Pallas kernels: 0 us -> 239 us
  matrix products: 781 us -> 600 us
  local copies, waits for them, and re-layouts: 138 us -> 28.8 us
  waiting for transfers between devices: 524 us -> 448 us
    dot_general x119 -> x0, starting transfers between devices: 926 us -> none  [the longest x51 377 us: matmul(): jnp.dot(a, w, preferred_element_type=jnp.float32).astype(jnp.bfloat16)]
    dot_general x119 -> x0, waiting for transfers between devices: 524 us -> none  [the longest x51 235 us: matmul(): jnp.dot(a, w, preferred_element_type=jnp.float32).astype(jnp.bfloat16)]
    reduce_scatter x0 -> x6, waiting for transfers between devices: none -> 448 us  [body(): lax.psum_scatter(t.astype(BF), 'dp', scatter_dimension=0, tiled=True)]
    pallas_call x0 -> x1, Pallas kernels: none -> 239 us  [gather_all(): pl.pallas_call(kernel, out_shape=[jax.ShapeDtypeStruct((2, 2, 2, 2, *s.sh...]
    dot_general x96 -> x0, other arithmetic: 217 us -> none
    dot_general x66 -> x17, matrix products: 781 us -> 600 us  [dot(): return lax.dot_general(a, b, (dims, ((), ())), preferred_element_type=F32)]
    add_any x3 -> x0, other arithmetic: 62.8 us -> none  [the longest x1 38 us: layer(): jax.nn.silu(gate) * up]
    unnamed x70 -> x37, local copies, waits for them, and re-layouts: 85.7 us -> 25.7 us
  transfers between devices with their start and end apart: 124 -> 6, of which waited for: 60 -> 4; matrix products, arithmetic and copies ran while one was open for 41% -> 22% of each run, Pallas kernels for 0% -> 0%
where the time goes in v1:
time: 1380 us; the launch traced here: 1370 us
  matrix products  600 us (43%)
  waiting for transfers between devices  448 us (32%)
  Pallas kernels  239 us (17%)
  other arithmetic  36.1 us (3%)
  local copies, waits for them, and re-layouts  28.8 us (2%)
  between operations  14.6 us (1%)
    dot_general x17, matrix products, dot(): return lax.dot_general(a, b, (dims, ((), ())), preferred_element_type=F32)  600 us
    reduce_scatter x6, waiting for transfers between devices, body(): lax.psum_scatter(t.astype(BF), 'dp', scatter_dimension=0, tiled=True)  448 us
    pallas_call x1, Pallas kernels, gather_all(): pl.pallas_call(kernel, out_shape=[jax.ShapeDtypeStruct((2, 2, 2, 2, *s.sh...  239 us
  transfers between devices with their start and end apart: 6, of which 4 were waited for; matrix products, arithmetic and copies ran while one was open for 22% of the time, Pallas kernels for 0%

profile of v1, /device:TPU:0, one launch (start us, length us, event | category | flops | bytes accessed | tf_op | source)
XLA Modules:
  0.0 1366.5 jit_solution(15188370710593406799)
XLA Ops:
  8.7 7.9 copy.10
  16.6 3.7 fusion.12
  21.0 1.6 slice_bitcast_fusion.1
  22.6 238.5 %gather_all.1 = (bf16[2,2,2,2,80,4480]{5,4,3,2,1,0:T(8,128)(2,1)}, bf16[2,2,2,2,80,4480]{5,4,3,2,1,0:T(8,128)(2,1)}, bf16[2,2,2,2,280,1280]{5,4,3,2,1,0:T(8,128)...) custom-call(bf16[80,4480]{1,0:T(8,128)(2,1)S(1)} %get-tuple-element., ...), custom_call_target="tpu_custom_call" | custom-call | tf_op jit(solution)/shard_map/gather_all/pallas_call | solution.py:71
  261.2 30.8 %fusion.38 = f32[2048,4480]{0,1:T(8,128)} fusion(bf16[1280,4480]{1,0:T(8,128)(2,1)} %bitcast.94, bf16[1,2048,1280]{2,1,0:T(8,128)(2,1)S(1)} %bitcast.85, f32[2048]{0:T(1024)S(1)} %add_rsqrt_fusion.1), kind=kOutput, calls=%fused_computation.62 | convolution fusion | flops 23495966720 | bytes 53420032 | tf_op jit(solution)/shard_map/dot_general | solution.py:91
  292.0 45.6 %multiply_convert_fusion.1 = (bf16[2048,4480]{0,1:T(8,128)(2,1)}, f32[2048,4480]{0,1:T(8,128)}) fusion(f32[2048,4480]{0,1:T(8,128)} %fusion.38, bf16[1280,4480]{1,0:T(8,128)(2,1)} %bitcast.96, bf16[1,2048,1280]{2,1,0:T(8,128)(2,1)} %param.5, f32[2048]{0:T(1024)S(1)} %add_rsqrt_fusion.1), kind=kOutput, calls=%fused_computation.13 | convolution fusion | flops 23551016960 | bytes 108470272 | tf_op jit(solution)/shard_map/dot_general | solution.py:91
  337.6 33.1 %fusion.15 = (f32[2048]{0:T(1024)S(1)}, bf16[2048,1280]{0,1:T(8,128)(2,1)}) fusion(bf16[2048,4480]{0,1:T(8,128)(2,1)} %get-tuple-element.30, bf16[4480,1280]{1,0:T(8,128)(2,1)} %bitcast.98, bf16[1,2048,1280]{1,2,0:T(8,128)(2,1)} %copy.10), kind=kOutput, calls=%fused_computation.41 | convolution fusion | flops 23501207552 | bytes 40312832 | tf_op jit(solution)/shard_map/dot_general | solution.py:91
  371.3 8.0 copy.9
  379.4 31.1 %convolution_convert_fusion.7 = bf16[4480,2048]{1,0:T(8,128)(2,1)} fusion(bf16[4480,1280]{1,0:T(8,128)(2,1)} %bitcast.104, bf16[1,2048,1280]{2,1,0:T(8,128)(2,1)} %param.6), kind=kOutput, calls=%fused_computation.23 | convolution fusion | flops 23497277440 | bytes 35061760 | tf_op jit(solution)/shard_map/dot_general | solution.py:91
  410.5 29.7 %fusion.32 = f32[2048,4480]{0,1:T(8,128)} fusion(bf16[1280,4480]{1,0:T(8,128)(2,1)} %bitcast.100, bf16[2048,1280]{0,1:T(8,128)(2,1)S(1)} %bitcast.87, f32[2048]{0:T(1024)S(1)} %add_rsqrt_fusion), kind=kOutput, calls=%fused_computation.59 | convolution fusion | flops 23495966720 | bytes 53420032 | tf_op jit(solution)/shard_map/dot_general | solution.py:91
  440.2 59.0 %fusion.4 = (bf16[2048,4480]{0,1:T(8,128)(2,1)}, bf16[2048,4480]{0,1:T(8,128)(2,1)}, f32[2048,4480]{0,1:T(8,128)}) fusion(bf16[4480,2048]{1,0:T(8,128)(2,1)} %convolution_convert_fusion.7, f32[2048,4480]{0,1:T(8,128)} %fusion.32, bf16[1280,4480]{1,0:T(8,128)(2,1)} %bitcast.102, bf16[2048,1280]{0,1:T(8,128)(2,1)} %get-tuple-element.33, ...), kind=kOutput, calls=%fused_computation.8 | convolution fusion | flops 23624417280 | bytes 145170432 | tf_op jit(solution)/shard_map/dot_general | solution.py:91
  499.2 32.1 %convolution_convert_fusion.11 = bf16[2048,1280]{0,1:T(8,128)(2,1)} fusion(bf16[1280,4480]{1,0:T(8,128)(2,1)} %bitcast.103, bf16[2048,4480]{0,1:T(8,128)(2,1)} %get-tuple-element.23), kind=kOutput, calls=%fused_computation.48 | convolution fusion | flops 23490723840 | bytes 35061760 | tf_op jit(solution)/shard_map/dot_general | solution.py:91
  531.3 30.4 %fusion.17 = (f32[2048]{0:T(1024)S(1)}, bf16[2048,1280]{0,1:T(8,128)(2,1)}) fusion(bf16[2048,1280]{0,1:T(8,128)(2,1)S(1)} %copy-done, bf16[2048,1280]{0,1:T(8,128)(2,1)} %convolution_convert_fusion.11, bf16[1280,4480]{1,0:T(8,128)(2,1)S(1)} %bitcast.101, bf16[2048,4480]{0,1:T(8,128)(2,1)} %get-tuple-element.22), kind=kOutput, calls=%fused_computation.43 | convolution fusion | flops 23503828992 | bytes 45555712 | tf_op jit(solution)/shard_map/dot_general | solution.py:91
  561.7 12.3 fusion.25
  574.0 29.7 %convolution_convert_fusion.6 = bf16[4480,1280]{1,0:T(8,128)(2,1)} fusion(bf16[2048,4480]{0,1:T(8,128)(2,1)} %get-tuple-element.30, bf16[2048,1280]{0,1:T(8,128)(2,1)} %fusion.25), kind=kOutput, calls=%fused_computation.22 | convolution fusion | flops 23493836800 | bytes 35061760 | tf_op jit(solution)/shard_map/dot_general | solution.py:91
  603.8 38.9 %convolution_convert_fusion.5 = bf16[4480,1280]{1,0:T(8,128)(2,1)} fusion(f32[2048,4480]{0,1:T(8,128)} %get-tuple-element.34, f32[2048,4480]{0,1:T(8,128)} %fusion.32, bf16[1,2048,1280]{2,1,0:T(8,128)(2,1)} %param.6), kind=kOutput, calls=%fused_computation.21 | convolution fusion | flops 23548887040 | bytes 90112000 | tf_op jit(solution)/shard_map/dot_general | solution.py:91
  642.8 31.3 %convolution_convert_fusion = bf16[1280,4480]{1,0:T(8,128)(2,1)} fusion(bf16[2048,4480]{0,1:T(8,128)(2,1)} %get-tuple-element.23, bf16[2048,1280]{0,1:T(8,128)(2,1)} %get-tuple-element.33, f32[2048]{0:T(1024)S(1)} %add_rsqrt_fusion), kind=kOutput, calls=%fused_computation.16 | convolution fusion | flops 23501701120 | bytes 35069952 | tf_op jit(solution)/shard_map/dot_general | solution.py:91
  674.1 49.8 %fusion.1 = (bf16[2048,4480]{0,1:T(8,128)(2,1)}, bf16[2048,4480]{0,1:T(8,128)(2,1)}) fusion(f32[2048,4480]{0,1:T(8,128)} %get-tuple-element.31, f32[2048,4480]{0,1:T(8,128)} %fusion.38, bf16[4480,1280]{1,0:T(8,128)(2,1)} %bitcast.99, bf16[2048,1280]{0,1:T(8,128)(2,1)} %fusion.25), kind=kOutput, calls=%fused_computation.3 | convolution fusion | flops 23625728000 | bytes 126812160 | tf_op jit(solution)/shard_map/dot_general | solution.py:91
  724.0 31.3 %convolution_convert_fusion.1 = bf16[1280,4480]{1,0:T(8,128)(2,1)} fusion(bf16[2048,4480]{0,1:T(8,128)(2,1)} %get-tuple-element.21, bf16[1,2048,1280]{1,2,0:T(8,128)(2,1)} %copy.10, f32[2048]{0:T(1024)S(1)} %copy-done.5), kind=kOutput, calls=%fused_computation.17 | convolution fusion | flops 23501701120 | bytes 35069952 | tf_op jit(solution)/shard_map/dot_general | solution.py:91
  756.0 31.6 %convolution_convert_fusion.2 = bf16[1280,4480]{1,0:T(8,128)(2,1)} fusion(bf16[2048,4480]{0,1:T(8,128)(2,1)} %get-tuple-element.22, bf16[2048,1280]{0,1:T(8,128)(2,1)} %get-tuple-element.33, f32[2048]{0:T(1024)S(1)} %copy-done.7), kind=kOutput, calls=%fused_computation.18 | convolution fusion | flops 23501701120 | bytes 35069952 | tf_op jit(solution)/shard_map/dot_general | solution.py:91
  787.6 31.6 %convolution_convert_fusion.3 = bf16[1280,4480]{1,0:T(8,128)(2,1)} fusion(bf16[2048,4480]{0,1:T(8,128)(2,1)} %get-tuple-element.20, bf16[1,2048,1280]{1,2,0:T(8,128)(2,1)} %copy.10, f32[2048]{0:T(1024)S(1)} %copy-done.5), kind=kOutput, calls=%fused_computation.19 | convolution fusion | flops 23501701120 | bytes 35069952 | tf_op jit(solution)/shard_map/dot_general | solution.py:91
  819.2 31.0 %convolution_convert_fusion.9 = bf16[2048,1280]{0,1:T(8,128)(2,1)S(1)} fusion(bf16[1280,4480]{1,0:T(8,128)(2,1)} %bitcast.97, bf16[2048,4480]{0,1:T(8,128)(2,1)} %get-tuple-element.21), kind=kOutput, calls=%fused_computation.46 | convolution fusion | flops 23490723840 | bytes 35061760 | tf_op jit(solution)/shard_map/dot_general | solution.py:91
  850.2 33.2 %fusion.13 = (f32[2048]{0:T(1024)S(1)}, bf16[2048,1280]{0,1:T(8,128)(2,1)}) fusion(bf16[1,2048,1280]{1,2,0:T(8,128)(2,1)S(1)} %bitcast.83, bf16[2048,1280]{0,1:T(8,128)(2,1)S(1)} %convolution_convert_fusion.9, bf16[1280,4480]{1,0:T(8,128)(2,1)} %bitcast.95, bf16[2048,4480]{0,1:T(8,128)(2,1)} %get-tuple-element.20), kind=kOutput, calls=%fused_computation.39 | convolution fusion | flops 23503828992 | bytes 45555712 | tf_op jit(solution)/shard_map/dot_general | solution.py:91
  883.4 12.3 fusion.24
  895.7 7.9 copy.22
  903.6 2.6 pad_maximum_fusion.2
  906.1 71.4 %reduce-scatter.13.cloned.1.call-done = bf16[80,4480]{1,0:T(8,128)(2,1)} async-done(((bf16[1280,4480]{1,0:T(8,128)(2,1)}), bf16[80,4480]{1,0:T(8,128)(2,1)}) %reduce-scatter.13.cloned.1.call-update) | async-done | bytes 716816 | tf_op jit(solution)/shard_map/reduce_scatter | solution.py:113
  977.6 126.4 %reduce-scatter.11.cloned.1.call-done = bf16[80,4480]{1,0:T(8,128)(2,1)} async-done(((bf16[1280,4480]{1,0:T(8,128)(2,1)}), bf16[80,4480]{1,0:T(8,128)(2,1)}) %reduce-scatter.11.cloned.1.call-update) | async-done | bytes 716816 | tf_op jit(solution)/shard_map/reduce_scatter | solution.py:113
  1104.0 2.6 pad_maximum_fusion.1
  1106.6 123.9 %reduce-scatter.9.cloned.1.call-done = bf16[80,4480]{1,0:T(8,128)(2,1)} async-done(((bf16[1280,4480]{1,0:T(8,128)(2,1)}), bf16[80,4480]{1,0:T(8,128)(2,1)}) %reduce-scatter.9.cloned.1.call-update) | async-done | bytes 716816 | tf_op jit(solution)/shard_map/reduce_scatter | solution.py:113
  1230.4 126.4 %reduce-scatter.7.cloned.1.call-done = bf16[80,4480]{1,0:T(8,128)(2,1)} async-done(((bf16[1280,4480]{1,0:T(8,128)(2,1)}), bf16[80,4480]{1,0:T(8,128)(2,1)}) %reduce-scatter.7.cloned.1.call-update) | async-done | bytes 716816 | tf_op jit(solution)/shard_map/reduce_scatter | solution.py:113
  1356.9 2.6 pad_maximum_fusion
  (56 shorter events, 3.8 us)
Async XLA Ops:
  7.2 13.8 %copy-start.1 = (bf16[2,80,4480]{2,1,0:T(8,128)(2,1)S(1)}, bf16[2,80,4480]{2,1,0:T(8,128)(2,1)}, u32[]{:S(2)}) copy-start(bf16[2,80,4480]{2,1,0:T(8,128)(2,1)} %param.8) | copy-start | bytes 4300804
  7.2 896.4 %reduce-scatter.15.cloned.1.call-start = ((), (), s32[]{:S(2)}) async-start(), calls=%async_computation.10 | async-start | bytes 12185600 | tf_op jit(solution)/shard_map/reduce_scatter | solution.py:113
  16.6 244.5 %slice-start.2 = ((s8[5242880]{0:T(1024)(128)(4,1)}), s8[4194304]{0:T(1024)(128)(4,1)S(1)}, s32[]{:S(2)}) async-start(s8[5242880]{0:T(1024)(128)(4,1)} %bitcast.84), calls=%async_computation.14 | async-start | bytes 8388608
  20.4 0.6 copy-start.2
  21.0 271.0 %copy-start.4 = (f32[2048]{0:T(1024)}, f32[2048]{0:T(1024)S(1)}, u32[]{:S(2)}) copy-start(f32[2048]{0:T(1024)S(1)} %add_rsqrt_fusion.1) | copy-start | bytes 24580
  21.0 240.2 %slice-start.3 = ((s8[5242880]{0:T(1024)(128)(4,1)}), s8[1048576]{0:T(1024)(128)(4,1)S(1)}, s32[]{:S(2)}) async-start(s8[5242880]{0:T(1024)(128)(4,1)} %bitcast.84), calls=%async_computation.15 | async-start | bytes 2097152
  370.7 0.6 copy-start.8
  371.3 271.5 %copy-start.6 = (f32[2048]{0:T(1024)}, f32[2048]{0:T(1024)S(1)}, u32[]{:S(2)}) copy-start(f32[2048]{0:T(1024)S(1)} %add_rsqrt_fusion) | copy-start | bytes 24580
  371.3 39.2 %slice-start.4 = ((s8[5242880]{0:T(1024)(128)(4,1)}), s8[1048576]{0:T(1024)(128)(4,1)S(1)}, s32[]{:S(2)}) async-start(s8[5242880]{0:T(1024)(128)(4,1)} %bitcast.86), calls=%async_computation.16 | async-start | bytes 2097152
  379.4 31.1 %slice-start.5 = ((s8[5242880]{0:T(1024)(128)(4,1)}), s8[4194304]{0:T(1024)(128)(4,1)S(1)}, s32[]{:S(2)}) async-start(s8[5242880]{0:T(1024)(128)(4,1)} %bitcast.86), calls=%async_computation.17 | async-start | bytes 8388608
  499.2 32.1 %copy-start = (bf16[2048,1280]{0,1:T(8,128)(2,1)S(1)}, bf16[2048,1280]{0,1:T(8,128)(2,1)}, u32[]{:S(2)}) copy-start(bf16[2048,1280]{0,1:T(8,128)(2,1)} %get-tuple-element.33) | copy-start | bytes 15728644
  499.2 32.1 %copy-start.10 = (bf16[2,2,2,2,80,4480]{5,4,3,2,1,0:T(8,128)(2,1)S(1)}, bf16[2,2,2,2,80,4480]{5,4,3,2,1,0:T(8,128)(2,1)}, u32[]{:S(2)}) copy-start(bf16[2,2,2,2,80,4480]{5,4,3,2,1,0:T(8,128)(2,1)} %get-tuple-element.15) | copy-start | bytes 34406404
  531.3 30.4 %copy-start.9 = (f32[2048]{0:T(1024)S(1)}, f32[2048]{0:T(1024)}, u32[]{:S(2)}) copy-start(f32[2048]{0:T(1024)} %copy-done.8) | copy-start | bytes 24580
  603.8 299.8 %reduce-scatter.17.cloned.1.call-start = ((), (), s32[]{:S(2)}) async-start(), calls=%async_computation.11 | async-start | bytes 12185600 | tf_op jit(solution)/shard_map/reduce_scatter | solution.py:113
  642.7 334.8 %reduce-scatter.13.cloned.1.call-start = ((), (), s32[]{:S(2)}) async-start(), calls=%async_computation.9 | async-start | bytes 12185600 | tf_op jit(solution)/shard_map/reduce_scatter | solution.py:113
  674.1 429.9 %reduce-scatter.11.cloned.1.call-start = ((), (), s32[]{:S(2)}) async-start(), calls=%async_computation.8 | async-start | bytes 12185600 | tf_op jit(solution)/shard_map/reduce_scatter | solution.py:113
  674.1 49.8 %copy-start.5 = (f32[2048]{0:T(1024)S(1)}, f32[2048]{0:T(1024)}, u32[]{:S(2)}) copy-start(f32[2048]{0:T(1024)} %copy-done.4) | copy-start | bytes 24580
  755.3 0.7 copy-start.7
  755.3 475.1 %reduce-scatter.9.cloned.1.call-start = ((), (), s32[]{:S(2)}) async-start(), calls=%async_computation.7 | async-start | bytes 12185600 | tf_op jit(solution)/shard_map/reduce_scatter | solution.py:113
  787.6 569.3 %reduce-scatter.7.cloned.1.call-start = ((), (), s32[]{:S(2)}) async-start(), calls=%async_computation.6 | async-start | bytes 12185600 | tf_op jit(solution)/shard_map/reduce_scatter | solution.py:113
  819.2 31.0 %slice-start = ((s8[5242880]{0:T(1024)(128)(4,1)}), s8[1048576]{0:T(1024)(128)(4,1)S(1)}, s32[]{:S(2)}) async-start(s8[5242880]{0:T(1024)(128)(4,1)} %bitcast.82), calls=%async_computation.12 | async-start | bytes 2097152
  819.2 31.0 %slice-start.1 = ((s8[5242880]{0:T(1024)(128)(4,1)}), s8[4194304]{0:T(1024)(128)(4,1)S(1)}, s32[]{:S(2)}) async-start(s8[5242880]{0:T(1024)(128)(4,1)} %bitcast.82), calls=%async_computation.13 | async-start | bytes 8388608
  850.2 33.2 %copy-start.3 = (f32[2048]{0:T(1024)S(1)}, f32[2048]{0:T(1024)}, u32[]{:S(2)}) copy-start(f32[2048]{0:T(1024)} %copy-done.2) | copy-start | bytes 24580
Sparse Core Ops, SparseCore 0:
  603.9 120.4 reduce-scatter.14
  726.7 124.2 reduce-scatter.16
  853.2 124.2 reduce-scatter.12
  979.7 124.2 reduce-scatter.10
  1106.1 124.2 reduce-scatter.8
  1232.6 124.2 reduce-scatter.6
